TPU v7x, 32 devices: a whole 2x2x4 slice. The times are simulated.
32 devices in a mesh: ctx: 4 (over z), head: 8 (over y, x, core).
Axes of the slice: x: 2, y: 2, z: 4, core: 2. Of those that a mesh axis runs over, the one named last changes fastest.
Arguments:
- video: bfloat16 [3072, 4096], P('ctx', 'head'), may hold values from -6 to 6
- audio: bfloat16 [384, 2048], P('ctx', 'head'), may hold values from -6 to 6
- video_gain: float32 [4096], P('head'), may hold values from 0.1 to 1.9
- audio_gain: float32 [2048], P('head'), may hold values from 0.1 to 1.9
- video_qkv: bfloat16 [4096, 3, 4096], P(None, None, 'head'), as said below
- video_cross: bfloat16 [4096, 3, 2048], P(None, None, 'head'), as said below
- audio_cross: bfloat16 [2048, 3, 2048], P(None, None, 'head'), as said below
- video_out: bfloat16 [4096, 4096], P('head'), may hold values from -0.09375 to 0.09375
- cross_video_out: bfloat16 [2048, 4096], P('head'), may hold values from -0.125 to 0.125
- cross_audio_out: bfloat16 [2048, 2048], P('head'), may hold values from -0.125 to 0.125
Outputs:
- video_result: bfloat16 [3072, 4096], P('ctx', 'head')
- audio_result: bfloat16 [384, 2048], P('ctx', 'head')
Inputs may be any that keep to these rules, and one draw needn't show every extreme that they name: `video_qkv`: entries lie within -32 / sqrt(4096) and 32 / sqrt(4096). `video_cross`: entries lie within -32 / sqrt(4096) and 32 / sqrt(4096). `audio_cross`: entries lie within -32 / sqrt(2048) and 32 / sqrt(2048).
All inputs are finite; a program needn't handle non-finite values.
Results may differ from a plain program's by a relative error of at most 0.014.
The roundings to bfloat16 on the way count: a program that leaves them out, or rounds other values in their place, can miss the bound.
Values may be sent and summed in bfloat16 or wider, within the bound.
A program may use at most 128 MiB of HBM per device.

v0:
```python
import jax
import jax.numpy as jnp
from jax import lax
from jax.sharding import PartitionSpec as P

HD = 128


EPSILON = 1e-06


def split_heads(matrix):
    return matrix.reshape(matrix.shape[0], -1, HD).transpose(1, 0, 2)


def join_heads(blocks):
    return blocks.transpose(1, 0, 2).reshape(blocks.shape[1], -1)


def attend(queries, keys, values):
    scale = HD ** (-0.5)

    def one_head(operands):
        query_block, key_block, value_block = operands
        scores = jnp.dot(query_block, key_block.T, preferred_element_type=jnp.float32) * scale
        highest = jnp.max(scores, axis=1, keepdims=True)
        weights = jnp.exp(scores - highest)
        totals = jnp.sum(weights, axis=1, keepdims=True)
        return (
            jnp.dot(weights.astype(jnp.bfloat16), value_block, preferred_element_type=jnp.float32)
            / totals
        )

    blocks = lax.map(one_head, (split_heads(queries), split_heads(keys), split_heads(values)))
    return join_heads(blocks).astype(jnp.bfloat16)


def body(
    video,
    audio,
    video_gain,
    audio_gain,
    video_qkv,
    video_cross,
    audio_cross,
    video_out,
    cross_video_out,
    cross_audio_out,
):
    scale = HD ** (-0.5)
    video_wide = video.astype(jnp.float32)
    audio_wide = audio.astype(jnp.float32)
    video_squares, audio_squares = lax.psum(
        (jnp.sum(video_wide * video_wide, axis=1), jnp.sum(audio_wide * audio_wide, axis=1)), "head"
    )
    video_rate = lax.rsqrt(video_squares / video_qkv.shape[0] + EPSILON)
    audio_rate = lax.rsqrt(audio_squares / audio_cross.shape[0] + EPSILON)
    video_scaled = (video_wide * video_gain).astype(jnp.bfloat16)
    audio_scaled = (audio_wide * audio_gain).astype(jnp.bfloat16)
    self_weight = video_qkv.reshape(video_qkv.shape[0], -1)
    mixed_weight = video_cross.reshape(video_cross.shape[0], -1)
    audio_weight = audio_cross.reshape(audio_cross.shape[0], -1)
    self_width = video_qkv.shape[2]
    cross_width = video_cross.shape[2]
    video_rows = video.shape[0]
    segment = lax.all_gather(video_scaled, "head", axis=1, tiled=True)
    self_acc = jnp.dot(segment, self_weight, preferred_element_type=jnp.float32)
    mixed_acc = jnp.dot(segment, mixed_weight, preferred_element_type=jnp.float32)
    audio_acc = jnp.dot(
        lax.all_gather(audio_scaled, "head", axis=1, tiled=True),
        audio_weight,
        preferred_element_type=jnp.float32,
    )
    self_proj = (self_acc * video_rate[:, None]).astype(jnp.bfloat16)
    video_mixed = (mixed_acc * video_rate[:, None]).astype(jnp.bfloat16)
    audio_mixed = (audio_acc * audio_rate[:, None]).astype(jnp.bfloat16)
    query_heads = split_heads(self_proj[:, :self_width])
    local_heads = query_heads.shape[0]
    running_max = jnp.full((local_heads, video_rows), -1e30, jnp.float32)
    key_heads = split_heads(
        lax.all_gather(self_proj[:, self_width : 2 * self_width], "ctx", axis=0, tiled=True)
    )
    value_heads = split_heads(
        lax.all_gather(self_proj[:, 2 * self_width :], "ctx", axis=0, tiled=True)
    )
    scores = (
        jnp.einsum("hqd,hkd->hqk", query_heads, key_heads, preferred_element_type=jnp.float32)
        * scale
    )
    newest = jnp.maximum(running_max, jnp.max(scores, axis=2))
    weights = jnp.exp(scores - newest[:, :, None])
    running_sum = jnp.sum(weights, axis=2)
    running_acc = jnp.einsum(
        "hqk,hkd->hqd",
        weights.astype(jnp.bfloat16),
        value_heads,
        preferred_element_type=jnp.float32,
    )
    self_out = join_heads(running_acc / running_sum[:, :, None]).astype(jnp.bfloat16)
    audio_key_all, audio_value_all = (
        lax.all_gather(audio_mixed[:, cross_width : 2 * cross_width], "ctx", axis=0, tiled=True),
        lax.all_gather(audio_mixed[:, 2 * cross_width :], "ctx", axis=0, tiled=True),
    )
    video_cross_out = attend(video_mixed[:, :cross_width], audio_key_all, audio_value_all)
    queries_av = audio_mixed[:, :cross_width]
    keys_av = video_mixed[:, cross_width : 2 * cross_width]
    values_av = video_mixed[:, 2 * cross_width :]
    every_query = lax.all_gather(queries_av, "ctx", axis=0, tiled=True)
    scores = (
        jnp.einsum(
            "hqd,hkd->hqk",
            split_heads(every_query),
            split_heads(keys_av),
            preferred_element_type=jnp.float32,
        )
        * scale
    )
    highest = lax.pmax(jnp.max(scores, axis=2), "ctx")
    weights = jnp.exp(scores - highest[:, :, None])
    numerators = jnp.einsum(
        "hqk,hkd->hqd",
        weights.astype(jnp.bfloat16),
        split_heads(values_av),
        preferred_element_type=jnp.float32,
    )
    weight_totals = jnp.sum(weights, axis=2)
    own_numer, own_totals = (
        lax.psum_scatter(
            numerators.astype(jnp.bfloat16), "ctx", scatter_dimension=1, tiled=True
        ).astype(jnp.float32),
        lax.psum_scatter(
            weight_totals.astype(jnp.bfloat16), "ctx", scatter_dimension=1, tiled=True
        ).astype(jnp.float32),
    )
    audio_cross_out = join_heads(own_numer / own_totals[:, :, None]).astype(jnp.bfloat16)
    video_partial = jnp.dot(self_out, video_out, preferred_element_type=jnp.float32) + jnp.dot(
        video_cross_out, cross_video_out, preferred_element_type=jnp.float32
    )
    audio_partial = jnp.dot(audio_cross_out, cross_audio_out, preferred_element_type=jnp.float32)
    video_sum, audio_sum = (
        lax.psum_scatter(
            video_partial.astype(jnp.bfloat16), "head", scatter_dimension=1, tiled=True
        ).astype(jnp.float32),
        lax.psum_scatter(
            audio_partial.astype(jnp.bfloat16), "head", scatter_dimension=1, tiled=True
        ).astype(jnp.float32),
    )
    return (
        (video_wide + video_sum).astype(jnp.bfloat16),
        (audio_wide + audio_sum).astype(jnp.bfloat16),
    )


def solution(mesh):
    return jax.shard_map(
        body,
        mesh=mesh,
        in_specs=(
            P("ctx", "head"),
            P("ctx", "head"),
            P("head"),
            P("head"),
            P(None, None, "head"),
            P(None, None, "head"),
            P(None, None, "head"),
            P("head", None),
            P("head", None),
            P("head", None),
        ),
        out_specs=(P("ctx", "head"), P("ctx", "head")),
        check_vma=False,
    )
```

profile of v0, /device:TPU:0, one launch (start us, length us, event | category | flops | bytes accessed | tf_op | source)
XLA Modules:
  0.0 384.8 jit_solution(10939205836591211655)
XLA Ops:
  7.2 2.4 fusion.22
  9.7 4.8 %copy.41 = bf16[2048,3,256]{0,2,1:T(8,128)(2,1)} copy(bf16[2048,3,256]{2,0,1:T(8,128)(2,1)} %param.18) | data formatting | bytes 6291456 | tf_op args[6]
  14.5 8.8 %copy.39 = bf16[4096,3,256]{0,2,1:T(8,128)(2,1)} copy(bf16[4096,3,256]{2,0,1:T(8,128)(2,1)} %param.17) | data formatting | bytes 12582912 | tf_op args[5]
  23.3 17.2 %copy.35 = bf16[4096,3,512]{0,2,1:T(8,128)(2,1)} copy(bf16[4096,3,512]{2,0,1:T(8,128)(2,1)} %param.16) | data formatting | bytes 25165824 | tf_op args[4]
  40.6 16.5 %all-reduce = (f32[768]{0:T(1024)S(1)}, f32[96]{0:T(128)S(1)}) all-reduce(f32[768]{0:T(1024)S(1)} %get-tuple-element.50, f32[96]{0:T(128)S(1)} %get-tuple-element.56), channel_id=1, replica_groups=mesh['ctx'=4,'head'=8] {'head'}, use_global_device_ids=true, to_apply=%region_1.0 | all-reduce | flops 864 | bytes 6912 | tf_op jit(solution)/shard_map/psum | solution.py:53
  57.1 9.4 %all_gather.24 = bf16[96,2048]{1,0:T(8,128)(2,1)S(1)} all-gather(bf16[96,256]{1,0:T(8,128)(2,1)S(1)} %get-tuple-element.55), channel_id=1, replica_groups=mesh['ctx'=4,'head'=8] {'head'}, dimensions={1}, use_global_device_ids=true | all-gather | bytes 442368 | tf_op jit(solution)/shard_map/all_gather | solution.py:70
  66.5 3.0 fusion.34
  69.5 0.6 fusion.50
  70.1 13.8 %all_gather.27 = bf16[384,256]{1,0:T(8,128)(2,1)S(1)} all-gather(bf16[96,256]{1,0:T(8,128)(2,1)S(1)} %get-tuple-element.52), channel_id=1, replica_groups=mesh['ctx'=4,'head'=8] {'ctx'}, dimensions={0}, use_global_device_ids=true | all-gather | bytes 245760 | tf_op jit(solution)/shard_map/all_gather | solution.py:108
  84.0 9.1 %multiply_convert_fusion.1 = bf16[768,768]{0,1:T(8,128)(2,1)S(1)} fusion(bf16[768,4096]{1,0:T(8,128)(2,1)} %all-gather.4.cloned.1.call-done, bf16[4096,768]{0,1:T(8,128)(2,1)} %bitcast.128, f32[768]{0:T(1024)S(1)} %add_rsqrt_fusion), kind=kOutput, calls=%fused_computation.30 | convolution fusion | flops 4833017856 | bytes 13765632 | tf_op jit(solution)/shard_map/dot_general | solution.py:68
  93.1 0.9 copy.47
  94.1 0.2 copy.46
  94.3 1.9 multiply_reduce_fusion.1
  96.2 12.1 %pmax.7 = f32[2,384]{1,0:T(2,128)S(1)} all-reduce(f32[2,384]{1,0:T(2,128)S(1)} %get-tuple-element.59), channel_id=1, replica_groups=mesh['ctx'=4,'head'=8] {'ctx'}, use_global_device_ids=true, to_apply=%region_12.13 | all-reduce | flops 768 | bytes 6144 | tf_op jit(solution)/shard_map/pmax | solution.py:118
  108.2 2.2 fusion.19
  110.5 0.8 copy.50
  111.4 3.0 fusion.31
  114.4 0.2 all-gather.6.cloned.1.call-start
  114.6 14.8 %multiply_convert_fusion = bf16[768,1536]{1,0:T(8,128)(2,1)S(1)} fusion(bf16[768,4096]{1,0:T(8,128)(2,1)} %all-gather.4.cloned.1.call-done, bf16[4096,1536]{0,1:T(8,128)(2,1)} %bitcast.126, f32[768]{0:T(1024)S(1)} %add_rsqrt_fusion), kind=kOutput, calls=%fused_computation.22 | convolution fusion | flops 9666035712 | bytes 21236736 | tf_op jit(solution)/shard_map/dot_general | solution.py:67
  129.4 1.5 slice_bitcast_fusion
  130.9 0.5 all-gather.8.cloned.1.call-update
  131.5 14.6 %all_gather.26 = bf16[384,256]{1,0:T(8,128)(2,1)S(1)} all-gather(bf16[96,256]{1,0:T(8,128)(2,1)S(1)} %copy-done.6), channel_id=1, replica_groups=mesh['ctx'=4,'head'=8] {'ctx'}, dimensions={0}, use_global_device_ids=true | all-gather | bytes 245760 | tf_op jit(solution)/shard_map/all_gather | solution.py:102
  146.2 13.6 %all_gather.25 = bf16[384,256]{1,0:T(8,128)(2,1)S(1)} all-gather(bf16[96,256]{1,0:T(8,128)(2,1)S(1)} %copy-done.5), channel_id=1, replica_groups=mesh['ctx'=4,'head'=8] {'ctx'}, dimensions={0}, use_global_device_ids=true | all-gather | bytes 245760 | tf_op jit(solution)/shard_map/all_gather | solution.py:101
  159.8 0.7 bitcast_bitcast_fusion.6
  160.6 0.2 copy.40
  160.8 4.0 %while.10 = (s32[]{:T(128)}, bf16[2,768,128]{1,2,0:T(8,128)(2,1)S(1)}, bf16[2,768,128]{2,1,0:T(8,128)(2,1)S(1)}, bf16[2,384,128]{2,1,0:T(8,128)(2,1)S(1)}, bf16[2,384,128]{2,1,0:T(8,128)(2,1)}, /*index=5*/s32[]{:T(128)}) while((s32[]{:T(128)}, bf16[2,768,128]{1,2,0:T(8,128)(2,1)S(1)}, bf16[2,768,128]{2,1,0:T(8,128)(2,1)S(1)}, ...), condition=%wide.region_9.10_spmd, body=%wide.region_6.9_spmd.sunk | while | flops 152959488 | bytes 4931669 | solution.py:34
  160.8 0.3 fusion.77
  161.1 0.2 fusion.78
  161.3 1.3 fusion.79
  162.6 0.1 copy.89
  162.8 0.3 fusion.77
  163.1 0.2 fusion.78
  163.3 1.3 fusion.79
  164.8 0.8 copy.51
  165.7 2.4 convolution_convert_fusion
  168.1 0.3 reduce-scatter.7.cloned.1.call-start
  168.4 43.3 %all-gather.6.cloned.1.call-done = bf16[3072,512]{1,0:T(8,128)(2,1)} async-done(((bf16[768,512]{1,0:T(8,128)(2,1)}), bf16[3072,512]{1,0:T(8,128)(2,1)}) %all-gather.6.cloned.1.call-update) | async-done | bytes 3145744 | tf_op jit(solution)/shard_map/all_gather | solution.py:81
  211.7 17.0 %multiply_reduce_fusion = (f32[4,768]{1,0:T(4,128)S(1)}, f32[4,768,3072]{2,1,0:T(8,128)}) fusion(bf16[96,4,8,128]{3,2,1,0:T(8,128)(2,1)} %get-tuple-element.44, bf16[3072,512]{1,0:T(8,128)(2,1)} %all-gather.6.cloned.1.call-done), kind=kOutput, calls=%fused_computation.17 | convolution fusion | flops 2434790400 | bytes 41693184 | tf_op jit(solution)/shard_map/hqd,hkd->hqk/dot_general | solution.py:87
  228.7 16.2 %fusion.13 = f32[4,768]{1,0:T(4,128)S(1)} fusion(f32[4,768,3072]{2,1,0:T(8,128)} %get-tuple-element.58, f32[4,768]{1,0:T(4,128)S(1)} %broadcast_maximum_fusion), kind=kLoop, calls=%fused_computation.18 | loop fusion | flops 28308480 | bytes 37773312 | tf_op jit(solution)/shard_map/reduce_sum | solution.py:92
  244.9 30.3 %all-gather.8.cloned.1.call-done = bf16[3072,512]{1,0:T(8,128)(2,1)} async-done(((bf16[768,512]{1,0:T(8,128)(2,1)}), bf16[3072,512]{1,0:T(8,128)(2,1)}) %all-gather.8.cloned.1.call-update) | async-done | bytes 3145744 | tf_op jit(solution)/shard_map/all_gather | solution.py:84
  275.2 4.7 %copy.49 = bf16[3072,512]{0,1:T(8,128)(2,1)} copy(bf16[3072,512]{1,0:T(8,128)(2,1)} %all-gather.8.cloned.1.call-done) | data formatting | bytes 6291456 | tf_op jit(solution)/shard_map/reshape | solution.py:13
  279.9 15.8 %fusion.24 = bf16[768,4,128]{0,2,1:T(8,128)(2,1)S(1)} fusion(bf16[4,3072,128]{1,2,0:T(8,128)(2,1)} %bitcast.130, f32[4,768,3072]{2,1,0:T(8,128)} %get-tuple-element.58, f32[4,768]{1,0:T(4,128)S(1)} %broadcast_maximum_fusion, f32[768,4]{0,1:T(4,128)S(1)} %bitcast.138), kind=kOutput, calls=%fused_computation.39 | convolution fusion | flops 2445017088 | bytes 41705472 | tf_op jit(solution)/shard_map/hqk,hkd->hqd/dot_general | solution.py:93
  295.8 3.5 fusion.51
  299.3 4.6 %add_convert_fusion = bf16[768,4096]{1,0:T(8,128)(2,1)} fusion(f32[768,4096]{1,0:T(8,128)S(1)} %fusion.51, bf16[768,256]{0,1:T(8,128)(2,1)S(1)} %bitcast.134, bf16[256,4096]{1,0:T(8,128)(2,1)S(1)} %copy-done), kind=kOutput, calls=%fused_computation.21 | convolution fusion | flops 1616904192 | bytes 21364736 | tf_op jit(solution)/shard_map/dot_general | solution.py:136
  303.9 6.7 %reduce-scatter.11.cloned.1.call-done = bf16[96,256]{1,0:T(8,128)(2,1)} async-done(((bf16[96,2048]{1,0:T(8,128)(2,1)}), bf16[96,256]{1,0:T(8,128)(2,1)}) %reduce-scatter.11.cloned.1.call-update) | async-done | bytes 49168 | tf_op jit(solution)/shard_map/reduce_scatter | solution.py:144
  310.7 1.4 fusion.42
  312.1 63.6 %reduce-scatter.7.cloned.1.call-done = bf16[768,512]{1,0:T(8,128)(2,1)} async-done(((bf16[768,4096]{1,0:T(8,128)(2,1)}), bf16[768,512]{1,0:T(8,128)(2,1)}) %reduce-scatter.7.cloned.1.call-update) | async-done | bytes 786448 | tf_op jit(solution)/shard_map/reduce_scatter | solution.py:141
  375.7 2.2 fusion.23
  (41 shorter events, 0.8 us)
Async XLA Ops:
  7.2 292.1 %copy-start = (bf16[256,4096]{1,0:T(8,128)(2,1)S(1)}, bf16[256,4096]{1,0:T(8,128)(2,1)}, u32[]{:S(2)}) copy-start(bf16[256,4096]{1,0:T(8,128)(2,1)} %param.20) | copy-start | bytes 6291460
  7.2 76.8 %all-gather.4.cloned.1.call-start = ((), (), s32[]{:S(2)}) async-start(), calls=%async_computation.4 | async-start | bytes 7077888 | tf_op jit(solution)/shard_map/all_gather | solution.py:66
  9.6 155.2 %reduce-scatter.13.cloned.1.call-start = ((), (), s32[]{:S(2)}) async-start(), calls=%async_computation.10 | async-start | bytes 122880
  23.3 17.2 %copy-start.4 = (bf16[96,256]{1,0:T(8,128)(2,1)S(1)}, bf16[96,256]{1,0:T(8,128)(2,1)}, u32[]{:S(2)}) copy-start(bf16[96,256]{1,0:T(8,128)(2,1)} %param.13) | copy-start | bytes 147460
  23.3 17.2 %copy-start.7 = (f32[256]{0:T(256)S(1)}, f32[256]{0:T(256)}, u32[]{:S(2)}) copy-start(f32[256]{0:T(256)} %param.15) | copy-start | bytes 3076
  94.3 17.1 %copy-start.3 = (bf16[768,2,128]{2,0,1:T(8,128)(2,1)S(1)}, bf16[768,2,128]{2,0,1:T(8,128)(2,1)}, u32[]{:S(2)}) copy-start(bf16[768,2,128]{2,0,1:T(8,128)(2,1)} %copy.47) | copy-start | bytes 1179652
  111.3 54.4 %reduce-scatter.9.cloned.1.call-start = ((), (), s32[]{:S(2)}) async-start(), calls=%async_computation.8 | async-start | bytes 245760 | tf_op jit(solution)/shard_map/reduce_scatter | solution.py:128
  114.4 97.3 %all-gather.6.cloned.1.call-start = ((), (), s32[]{:S(2)}) async-start(), calls=%async_computation.5 | async-start | bytes 3932160 | tf_op jit(solution)/shard_map/all_gather | solution.py:81
  129.4 2.1 copy-start.6
  129.4 16.8 %copy-start.5 = (bf16[96,256]{1,0:T(8,128)(2,1)S(1)}, bf16[96,256]{1,0:T(8,128)(2,1)}, u32[]{:S(2)}) copy-start(bf16[96,256]{1,0:T(8,128)(2,1)} %get-tuple-element.54) | copy-start | bytes 147460
  130.9 144.3 %all-gather.8.cloned.1.call-start = ((), (), s32[]{:S(2)}) async-start(), calls=%async_computation.6 | async-start | bytes 3932160 | tf_op jit(solution)/shard_map/all_gather | solution.py:84
  131.5 179.2 %reduce-scatter.11.cloned.1.call-start = ((), (), s32[]{:S(2)}) async-start(), calls=%async_computation.9 | async-start | bytes 442368 | tf_op jit(solution)/shard_map/reduce_scatter | solution.py:144
  168.1 207.6 %reduce-scatter.7.cloned.1.call-start = ((), (), s32[]{:S(2)}) async-start(), calls=%async_computation.7 | async-start | bytes 7077888 | tf_op jit(solution)/shard_map/reduce_scatter | solution.py:141
  279.9 15.8 %copy-start.1 = (bf16[512,4096]{1,0:T(8,128)(2,1)S(1)}, bf16[512,4096]{1,0:T(8,128)(2,1)}, u32[]{:S(2)}) copy-start(bf16[512,4096]{1,0:T(8,128)(2,1)} %param.19) | copy-start | bytes 12582916
  303.9 71.8 %copy-start.2 = (bf16[768,512]{1,0:T(8,128)(2,1)S(1)}, bf16[768,512]{1,0:T(8,128)(2,1)}, u32[]{:S(2)}) copy-start(bf16[768,512]{1,0:T(8,128)(2,1)} %param.12) | copy-start | bytes 2359300
Sparse Core Ops, SparseCore 0:
  10.4 49.6 all-gather.3
  111.4 16.6 reduce-scatter.12
  130.4 18.3 reduce-scatter.8
  150.2 61.4 all-gather.5
  213.1 62.0 all-gather.7
  278.1 32.5 reduce-scatter.10
  314.1 61.6 reduce-scatter.6
where the time goes:
time: 386 us; the launch traced here: 385 us
  waiting for transfers between devices  145 us (38%)
  blocking collectives  80.1 us (21%)
  matrix products  78.3 us (20%)
  local copies, waits for them, and re-layouts  41.7 us (11%)
  other arithmetic  24.9 us (6%)
  between operations  14.3 us (4%)
    reduce_scatter x1, waiting for transfers between devices, body(): lax.psum_scatter(video_partial.astype(jnp.bfloat16), 'head', scatter_dime...  63.6 us
    all_gather x1, waiting for transfers between devices, body(): lax.all_gather(self_proj[:, self_width:2 * self_width], 'ctx', axis=0, ti...  43.3 us
    unnamed x22, local copies, waits for them, and re-layouts  33.9 us
    all_gather x1, waiting for transfers between devices, body(): lax.all_gather(self_proj[:, 2 * self_width:], 'ctx', axis=0, tiled=True)  30.3 us
    dot_general x1, matrix products, body(): jnp.einsum('hqd,hkd->hqk', query_heads, key_heads, preferred_element_type...  17 us
    psum x1, blocking collectives, body(): lax.psum((jnp.sum(video_wide * video_wide, axis=1), jnp.sum(audio_wide *...  16.5 us
    reduce_sum x1, other arithmetic, body(): running_sum = jnp.sum(weights, axis=2)  16.2 us
    dot_general x1, matrix products, body(): jnp.einsum('hqk,hkd->hqd', weights.astype(jnp.bfloat16), value_heads, pre...  15.8 us
  transfers between devices with their start and end apart: 7, of which 4 were waited for; matrix products, arithmetic and copies ran while one was open for 33% of the time, Pallas kernels for 0%

commit v1 on v0

--- a/solution.py
+++ b/solution.py
@@ -1,6 +1,11 @@
+import functools
+import math
+
 import jax
 import jax.numpy as jnp
 from jax import lax
+from jax.experimental import pallas as pl
+from jax.experimental.pallas import tpu as pltpu
 from jax.sharding import PartitionSpec as P
 
 HD = 128
@@ -35,7 +40,7 @@
     return join_heads(blocks).astype(jnp.bfloat16)
 
 
-def body(
+def plain_body(
     video,
     audio,
     video_gain,
@@ -151,7 +156,506 @@
     )
 
 
+MESH = pl.DeviceIdType.MESH
+F32 = jnp.float32
+BF16 = jnp.bfloat16
+VMEM_LIMIT = 60 * 1024 * 1024
+
+
+def greet(peers):
+    barrier = pltpu.get_barrier_semaphore()
+    for peer in peers:
+        pl.semaphore_signal(barrier, inc=1, device_id=peer, device_id_type=MESH)
+    pl.semaphore_wait(barrier, len(peers))
+
+
+def head_peer(me, flip):
+    low = me % 2
+    mid = (me // 2) % 2
+    high = me // 4
+    if flip & 1:
+        low = 1 - low
+    if flip & 2:
+        mid = 1 - mid
+    if flip & 4:
+        high = 1 - high
+    return high * 4 + mid * 2 + low
+
+
+def half_rows(rows):
+    return (rows // 2 + 15) // 16 * 16
+
+
+def gather_kernel(x_ref, sq_ref, out_ref, sqs_ref, send, recv, own_sem):
+    ctx = lax.axis_index("ctx")
+    me = lax.axis_index("head")
+    rows = x_ref.shape[0]
+    half = half_rows(rows)
+    top = pl.ds(0, half)
+    low = pl.ds(half, rows - half)
+    peer = [head_peer(me, flip) for flip in range(8)]
+    greet([(ctx, peer[flip]) for flip in range(1, 8)])
+
+    def copy(slot, flip, source, target):
+        return pltpu.make_async_remote_copy(
+            src_ref=source,
+            dst_ref=target,
+            send_sem=send.at[slot],
+            recv_sem=recv.at[slot],
+            device_id=(ctx, peer[flip]),
+            device_id_type=MESH,
+        )
+
+    squares = [copy(10 + flip, flip, sq_ref, sqs_ref.at[flip]) for flip in range(1, 8)]
+    x_top = copy(0, 2, x_ref.at[top], out_ref.at[me, top])
+    x_low = copy(1, 2, x_ref.at[low], out_ref.at[me, low])
+    y_low = copy(2, 4, x_ref.at[low], out_ref.at[me, low])
+    y_top = copy(3, 4, x_ref.at[top], out_ref.at[me, top])
+    side = copy(4, 1, x_ref, out_ref.at[me])
+    x_top.start()
+    y_low.start()
+    x_low.start()
+    y_top.start()
+    for square in squares:
+        square.start()
+    side.start()
+    own = pltpu.make_async_copy(x_ref, out_ref.at[me], own_sem.at[0])
+    own_square = pltpu.make_async_copy(sq_ref, sqs_ref.at[0], own_sem.at[1])
+    own.start()
+    own_square.start()
+    from_x = peer[2]
+    from_y = peer[4]
+    far = peer[6]
+    x_top.wait_recv()
+    far_top = copy(5, 4, out_ref.at[from_x, top], out_ref.at[from_x, top])
+    far_top.start()
+    y_low.wait_recv()
+    far_low = copy(6, 2, out_ref.at[from_y, low], out_ref.at[from_y, low])
+    far_low.start()
+    x_low.wait_recv()
+    side_x = copy(7, 1, out_ref.at[from_x], out_ref.at[from_x])
+    side_x.start()
+    y_top.wait_recv()
+    side_y = copy(8, 1, out_ref.at[from_y], out_ref.at[from_y])
+    side_y.start()
+    far_top.wait_recv()
+    side_top = copy(9, 1, out_ref.at[far, top], out_ref.at[far, top])
+    side_top.start()
+    far_low.wait_recv()
+    side_low = copy(10, 1, out_ref.at[far, low], out_ref.at[far, low])
+    side_low.start()
+    for one in (side, side_x, side_y, side_top, side_low):
+        one.wait_recv()
+    for square in squares:
+        square.wait_recv()
+    own.wait()
+    own_square.wait()
+    for one in squares + [
+        x_top, x_low, y_low, y_top, side, far_top, far_low, side_x, side_y, side_top, side_low
+    ]:
+        one.wait_send()
+
+
+def gather_blocks(block, squares):
+    return pl.pallas_call(
+        gather_kernel,
+        out_shape=(
+            jax.ShapeDtypeStruct((8,) + block.shape, block.dtype),
+            jax.ShapeDtypeStruct((8,) + squares.shape, squares.dtype),
+        ),
+        in_specs=[pl.BlockSpec(memory_space=pltpu.VMEM)] * 2,
+        out_specs=(pl.BlockSpec(memory_space=pl.ANY), pl.BlockSpec(memory_space=pl.ANY)),
+        scratch_shapes=[
+            pltpu.SemaphoreType.DMA((18,)),
+            pltpu.SemaphoreType.DMA((18,)),
+            pltpu.SemaphoreType.DMA((2,)),
+        ],
+        compiler_params=pltpu.CompilerParams(collective_id=0, has_side_effects=True),
+        name="gather_blocks",
+    )(block, squares)
+
+
+def scatter_kernel(part_ref, base_ref, out_ref, chip, x_in, y_in, x_last, y_last, send, recv):
+    ctx = lax.axis_index("ctx")
+    me = lax.axis_index("head")
+    rows = base_ref.shape[0]
+    half = half_rows(rows)
+    top = pl.ds(0, half)
+    low = pl.ds(half, rows - half)
+    peer = [head_peer(me, flip) for flip in range(8)]
+    greet([(ctx, peer[flip]) for flip in (1, 2, 4)])
+
+    def copy(slot, flip, source, target):
+        return pltpu.make_async_remote_copy(
+            src_ref=source,
+            dst_ref=target,
+            send_sem=send.at[slot],
+            recv_sem=recv.at[slot],
+            device_id=(ctx, peer[flip]),
+            device_id_type=MESH,
+        )
+
+    side = [copy(k, 1, part_ref.at[peer[2 * k + 1]], chip.at[k]) for k in range(4)]
+    for k in (3, 1, 2, 0):
+        side[k].start()
+
+    def add_chip(k):
+        side[k].wait_recv()
+        chip[k] = (chip[k].astype(F32) + part_ref[peer[2 * k]].astype(F32)).astype(BF16)
+
+    add_chip(3)
+    x_far = copy(4, 2, chip.at[3, top], x_in.at[1])
+    y_far = copy(5, 4, chip.at[3, low], y_in.at[1, pl.ds(0, rows - half)])
+    x_far.start()
+    y_far.start()
+    add_chip(1)
+    x_near = copy(6, 2, chip.at[1, top], x_in.at[0])
+    x_near.start()
+    add_chip(2)
+    y_near = copy(7, 4, chip.at[2, low], y_in.at[0, pl.ds(0, rows - half)])
+    y_near.start()
+    side[0].wait_recv()
+    x_far.wait_recv()
+    chip[2, :half] = (chip[2, :half].astype(F32) + x_in[1].astype(F32)).astype(BF16)
+    y_end = copy(8, 4, chip.at[2, top], y_last)
+    y_end.start()
+    y_far.wait_recv()
+    chip[1, half:] = (
+        chip[1, half:].astype(F32) + y_in[1, : rows - half].astype(F32)
+    ).astype(BF16)
+    x_end = copy(9, 2, chip.at[1, low], x_last.at[pl.ds(0, rows - half)])
+    x_end.start()
+    total = chip[0].astype(F32) + part_ref[me].astype(F32) + base_ref[...].astype(F32)
+    x_near.wait_recv()
+    y_near.wait_recv()
+    total_top = total[:half] + x_in[0].astype(F32)
+    total_low = total[half:] + y_in[0, : rows - half].astype(F32)
+    y_end.wait_recv()
+    out_ref[:half] = (total_top + y_last[...].astype(F32)).astype(BF16)
+    x_end.wait_recv()
+    out_ref[half:] = (total_low + x_last[: rows - half].astype(F32)).astype(BF16)
+    for one in side + [x_far, y_far, x_near, y_near, y_end, x_end]:
+        one.wait_send()
+
+
+def scatter_blocks(parts, base):
+    rows, width = base.shape
+    half = half_rows(rows)
+    return pl.pallas_call(
+        scatter_kernel,
+        out_shape=jax.ShapeDtypeStruct(base.shape, base.dtype),
+        in_specs=[pl.BlockSpec(memory_space=pltpu.VMEM)] * 2,
+        out_specs=pl.BlockSpec(memory_space=pltpu.VMEM),
+        scratch_shapes=[
+            pltpu.VMEM((4, rows, width), BF16),
+            pltpu.VMEM((2, half, width), BF16),
+            pltpu.VMEM((2, half, width), BF16),
+            pltpu.VMEM((half, width), BF16),
+            pltpu.VMEM((half, width), BF16),
+            pltpu.SemaphoreType.DMA((10,)),
+            pltpu.SemaphoreType.DMA((10,)),
+        ],
+        compiler_params=pltpu.CompilerParams(
+            collective_id=1, has_side_effects=True, vmem_limit_bytes=VMEM_LIMIT
+        ),
+        name="scatter_blocks",
+    )(parts, base)
+
+
+def project_kernel(heads, x_ref, w_ref, rate_ref, out_ref, total):
+    step = pl.program_id(0)
+    for plane in range(w_ref.shape[0]):
+        product = jnp.dot(x_ref[0], w_ref[plane], preferred_element_type=F32)
+
+        @pl.when(step == 0)
+        def _():
+            total[plane] = product
+
+        @pl.when(step > 0)
+        def _():
+            total[plane] += product
+
+    @pl.when(step == pl.num_programs(0) - 1)
+    def _():
+        for plane in range(w_ref.shape[0]):
+            for h in range(heads):
+                out_ref[h, plane] = (
+                    total[plane, :, h * HD : (h + 1) * HD] * rate_ref[...]
+                ).astype(BF16)
+
+
+def project(blocks, rows, weight, rate):
+    planes, _, width = weight.shape
+    depth = blocks.shape[2]
+    heads = width // HD
+    return pl.pallas_call(
+        functools.partial(project_kernel, heads),
+        grid=(blocks.shape[0],),
+        out_shape=jax.ShapeDtypeStruct((heads, planes, rows, HD), BF16),
+        in_specs=[
+            pl.BlockSpec((1, rows, depth), lambda b: (b, 0, 0)),
+            pl.BlockSpec((planes, depth, width), lambda b: (0, b, 0)),
+            pl.BlockSpec((rows, 1), lambda b: (0, 0)),
+        ],
+        out_specs=pl.BlockSpec((heads, planes, rows, HD), lambda b: (0, 0, 0, 0)),
+        scratch_shapes=[pltpu.VMEM((planes, rows, width), F32)],
+        compiler_params=pltpu.CompilerParams(
+            dimension_semantics=("arbitrary",), vmem_limit_bytes=VMEM_LIMIT
+        ),
+        cost_estimate=pl.CostEstimate(
+            flops=2 * planes * rows * width * depth * blocks.shape[0],
+            bytes_accessed=2 * planes * width * depth * blocks.shape[0],
+            transcendentals=0,
+        ),
+        name="project",
+    )(blocks, weight, rate)
+
+
+def contract_last(left, right):
+    return lax.dot_general(left, right, (((1,), (1,)), ((), ())), preferred_element_type=F32)
+
+
+def softmax_parts(query, keys, values):
+    scale = HD ** (-0.5)
+    scores = [contract_last(query, key) for key in keys]
+    highest = functools.reduce(
+        jnp.maximum, [jnp.max(score, axis=1, keepdims=True) for score in scores]
+    )
+    total = 0.0
+    mixed = 0.0
+    for score, value in zip(scores, values):
+        weight = jnp.exp((score - highest) * scale)
+        total = total + jnp.sum(weight, axis=1, keepdims=True)
+        mixed = mixed + jnp.dot(weight.astype(BF16), value, preferred_element_type=F32)
+    return mixed, total, highest * scale
+
+
+def attention_kernel(count, q_ref, *refs):
+    out_ref = refs[-1]
+    keys = [refs[i][0, 0] for i in range(count)]
+    values = [refs[count + i][0, 0] for i in range(count)]
+    mixed, total, _ = softmax_parts(q_ref[0, 0], keys, values)
+    out_ref[0] = (mixed / total).astype(BF16)
+
+
+def self_attention(queries, sources):
+    heads, _, rows, _ = queries.shape
+    tile = math.gcd(rows, 256)
+    count = len(sources)
+    keys_all = count * rows
+    return pl.pallas_call(
+        functools.partial(attention_kernel, count),
+        grid=(heads, rows // tile),
+        out_shape=jax.ShapeDtypeStruct((heads, rows, HD), BF16),
+        in_specs=[pl.BlockSpec((1, 1, tile, HD), lambda h, i: (h, 0, i, 0))]
+        + [pl.BlockSpec((1, 1, rows, HD), lambda h, i: (h, 1, 0, 0))] * count
+        + [pl.BlockSpec((1, 1, rows, HD), lambda h, i: (h, 2, 0, 0))] * count,
+        out_specs=pl.BlockSpec((1, tile, HD), lambda h, i: (h, i, 0)),
+        compiler_params=pltpu.CompilerParams(
+            dimension_semantics=("arbitrary", "arbitrary"), vmem_limit_bytes=VMEM_LIMIT
+        ),
+        cost_estimate=pl.CostEstimate(
+            flops=8 * heads * rows * keys_all * HD,
+            bytes_accessed=4 * heads * keys_all * HD,
+            transcendentals=heads * rows * keys_all,
+        ),
+        name="self_attention",
+    )(queries, *sources, *sources)
+
+
+def cross_kernel(count, video_ref, *refs):
+    audio = refs[:count]
+    out_ref, part_ref, stats_ref = refs[count:]
+    heads = video_ref.shape[0]
+    for h in range(heads):
+        at = [slice((plane * heads + h) * HD, (plane * heads + h + 1) * HD) for plane in range(3)]
+        mixed, total, _ = softmax_parts(
+            video_ref[h, 0], [one[:, at[1]] for one in audio], [one[:, at[2]] for one in audio]
+        )
+        out_ref[:, h * HD : (h + 1) * HD] = (mixed / total).astype(BF16)
+        for d in range(count):
+            mixed, total, highest = softmax_parts(
+                audio[d][:, at[0]], [video_ref[h, 1]], [video_ref[h, 2]]
+            )
+            part_ref[d, :, h * HD : (h + 1) * HD] = (mixed / total).astype(BF16)
+            lanes = lax.broadcasted_iota(jnp.int32, (mixed.shape[0], HD), 1)
+            stats_ref[d, h] = jnp.where(lanes < HD // 2, total, highest)
+
+
+def cross_attention(video_heads, audio_sources):
+    heads, _, rows, _ = video_heads.shape
+    count = len(audio_sources)
+    audio_rows = audio_sources[0].shape[0]
+    whole = pl.BlockSpec(memory_space=pltpu.VMEM)
+    return pl.pallas_call(
+        functools.partial(cross_kernel, count),
+        out_shape=(
+            jax.ShapeDtypeStruct((rows, heads * HD), BF16),
+            jax.ShapeDtypeStruct((count, audio_rows, heads * HD), BF16),
+            jax.ShapeDtypeStruct((count, heads, audio_rows, HD), F32),
+        ),
+        in_specs=[whole] * (1 + count),
+        out_specs=(whole, whole, whole),
+        compiler_params=pltpu.CompilerParams(vmem_limit_bytes=VMEM_LIMIT),
+        cost_estimate=pl.CostEstimate(
+            flops=16 * heads * rows * count * audio_rows * HD,
+            bytes_accessed=8 * rows * heads * HD,
+            transcendentals=2 * heads * rows * count * audio_rows,
+        ),
+        name="cross_attention",
+    )(video_heads, *audio_sources)
+
+
+def output_kernel(self_ref, cross_ref, audio_ref, w_self, w_cross, w_audio, out_ref):
+    rows = self_ref.shape[0]
+    out_ref[0, :rows] = (
+        jnp.dot(self_ref[...], w_self[...], preferred_element_type=F32)
+        + jnp.dot(cross_ref[...], w_cross[...], preferred_element_type=F32)
+    ).astype(BF16)
+    sound = jnp.dot(audio_ref[...], w_audio[...], preferred_element_type=F32).astype(BF16)
+    half = sound.shape[0] // 2
+    width = sound.shape[1]
+    out_ref[0, rows:, :width] = sound[:half]
+    out_ref[0, rows:, width:] = sound[half:]
+
+
+def output_parts(self_out, cross_out, audio_out, w_self, w_cross, w_audio):
+    rows, depth = self_out.shape
+    audio_rows, cross_depth = audio_out.shape
+    width = w_self.shape[1] // 8
+    audio_width = w_audio.shape[1] // 8
+    return pl.pallas_call(
+        output_kernel,
+        grid=(8,),
+        out_shape=jax.ShapeDtypeStruct((8, rows + audio_rows // 2, width), BF16),
+        in_specs=[
+            pl.BlockSpec((rows, depth), lambda n: (0, 0)),
+            pl.BlockSpec((rows, cross_depth), lambda n: (0, 0)),
+            pl.BlockSpec((audio_rows, cross_depth), lambda n: (0, 0)),
+            pl.BlockSpec((depth, width), lambda n: (0, n)),
+            pl.BlockSpec((cross_depth, width), lambda n: (0, n)),
+            pl.BlockSpec((cross_depth, audio_width), lambda n: (0, n)),
+        ],
+        out_specs=pl.BlockSpec((1, rows + audio_rows // 2, width), lambda n: (n, 0, 0)),
+        compiler_params=pltpu.CompilerParams(
+            dimension_semantics=("arbitrary",), vmem_limit_bytes=VMEM_LIMIT
+        ),
+        name="output_parts",
+    )(self_out, cross_out, audio_out, w_self, w_cross, w_audio)
+
+
+def pack(video_block, audio_block):
+    half = audio_block.shape[0] // 2
+    return jnp.concatenate(
+        [video_block, jnp.concatenate([audio_block[:half], audio_block[half:]], axis=1)], axis=0
+    )
+
+
+def square_tile(video_squares, audio_squares):
+    flat = jnp.concatenate([video_squares, audio_squares])
+    size = (flat.shape[0] + 1023) // 1024 * 1024
+    return jnp.pad(flat, (0, size - flat.shape[0])).reshape(-1, 128)
+
+
+def fast_body(
+    ctx_size,
+    video,
+    audio,
+    video_gain,
+    audio_gain,
+    video_qkv,
+    video_cross,
+    audio_cross,
+    video_out,
+    cross_video_out,
+    cross_audio_out,
+):
+    me = lax.axis_index("ctx")
+    rows = video.shape[0]
+    audio_rows = audio.shape[0]
+
+    def shift(value, distance):
+        ring = [(i, (i + distance) % ctx_size) for i in range(ctx_size)]
+        return lax.ppermute(value, "ctx", ring)
+
+    video_wide = video.astype(F32)
+    audio_wide = audio.astype(F32)
+    block = pack((video_wide * video_gain).astype(BF16), (audio_wide * audio_gain).astype(BF16))
+    squares = square_tile(
+        jnp.sum(video_wide * video_wide, axis=1), jnp.sum(audio_wide * audio_wide, axis=1)
+    )
+    blocks, every_square = gather_blocks(block, squares)
+    sums = jnp.sum(every_square, axis=0).reshape(-1)
+    video_rate = lax.rsqrt(sums[:rows] / video_qkv.shape[0] + EPSILON)[:, None]
+    audio_rate = lax.rsqrt(sums[rows : rows + audio_rows] / audio_cross.shape[0] + EPSILON)[:, None]
+
+    self_heads = project(blocks, rows, video_qkv.transpose(1, 0, 2), video_rate)
+    heads = self_heads.shape[0]
+    shares = self_heads.reshape((ctx_size, heads // ctx_size) + self_heads.shape[1:])
+
+    def share(stack, distance):
+        return lax.dynamic_index_in_dim(stack, (me + distance) % ctx_size, 0, keepdims=False)
+
+    sources = [share(shares, 0)] + [shift(share(shares, d), d) for d in range(1, ctx_size)]
+
+    audio_full = (
+        blocks[:, rows:, :]
+        .reshape(8, audio_rows // 2, 2, -1)
+        .transpose(2, 1, 0, 3)
+        .reshape(audio_rows, -1)
+    )
+    audio_mixed = jnp.concatenate(
+        [
+            (
+                jnp.dot(audio_full, audio_cross[:, plane, :], preferred_element_type=F32)
+                * audio_rate
+            ).astype(BF16)
+            for plane in range(3)
+        ],
+        axis=1,
+    )
+    audio_sources = [audio_mixed] + [shift(audio_mixed, d) for d in range(1, ctx_size)]
+    cross_heads = project(blocks, rows, video_cross.transpose(1, 0, 2), video_rate)
+    cross_out, parts, stats = cross_attention(cross_heads, audio_sources)
+    own_parts = jnp.stack([parts[0]] + [shift(parts[d], -d) for d in range(1, ctx_size)])
+    stats = jnp.stack([stats[..., 0], stats[..., HD - 1]], axis=1)
+    own_stats = jnp.stack([stats[0]] + [shift(stats[d], -d) for d in range(1, ctx_size)])
+    totals, highs = own_stats[:, 0], own_stats[:, 1]
+    shares_of = totals * jnp.exp(highs - jnp.max(highs, axis=0, keepdims=True))
+    shares_of = (shares_of / jnp.sum(shares_of, axis=0, keepdims=True)).transpose(0, 2, 1)
+    split_parts = own_parts.astype(F32).reshape(ctx_size, audio_rows, -1, HD)
+    audio_cross_out = (
+        jnp.sum(split_parts * shares_of[..., None], axis=0).reshape(audio_rows, -1).astype(BF16)
+    )
+
+    results = [None] * ctx_size
+    for d in list(range(1, ctx_size)) + [0]:
+        result = self_attention(sources[d], sources)
+        results[d] = shift(result, -d) if d else result
+    doubled = jnp.concatenate(results + results, axis=0)
+    group = heads // ctx_size
+    ordered = lax.dynamic_slice_in_dim(
+        doubled, ((ctx_size - me) % ctx_size) * group, heads, axis=0
+    )
+    self_out = join_heads(ordered)
+    partial = output_parts(
+        self_out, cross_out, audio_cross_out, video_out, cross_video_out, cross_audio_out
+    )
+    done = scatter_blocks(partial, pack(video, audio))
+    sound = done[rows:]
+    width = audio.shape[1]
+    return done[:rows], jnp.concatenate([sound[:, :width], sound[:, width:]], axis=0)
+
+
 def solution(mesh):
+    ctx_size = mesh.shape["ctx"]
+
+    def body(*operands):
+        heads = operands[4].shape[2] // HD
+        if mesh.shape["head"] == 2**3 and heads % ctx_size == 0:
+            return fast_body(ctx_size, *operands)
+        return plain_body(*operands)
+
     return jax.shard_map(
         body,
         mesh=mesh,

time: 386 us -> 228 us (0.59)
  Pallas kernels: 0 us -> 156 us
  waiting for transfers between devices: 145 us -> 9.59 us
  blocking collectives: 80.1 us -> 0 us
  matrix products: 78.3 us -> 4.6 us
  starting transfers between devices: 0.69 us -> 35 us
  local copies, waits for them, and re-layouts: 41.7 us -> 14.7 us
  other arithmetic: 24.9 us -> 6.31 us
  between operations: 14.3 us -> 0.95 us
    pallas_call x0 -> x10, Pallas kernels: none -> 156 us  [the longest x2 38.5 us: project(): pl.pallas_call(functools.partial(project_kernel, heads), grid=(blocks.sha...]
    dot_general x14 -> x3, matrix products: 78.3 us -> 4.6 us  [fast_body(): jnp.dot(audio_full, audio_cross[:, plane, :], preferred_element_type=F32)]
    all_gather x3 -> x0, waiting for transfers between devices: 73.7 us -> none  [the longest x1 43.3 us: body(): lax.all_gather(self_proj[:, self_width:2 * self_width], 'ctx', axis=0, ti...]
    reduce_scatter x3 -> x0, waiting for transfers between devices: 70.3 us -> none  [the longest x1 63.6 us: body(): lax.psum_scatter(video_partial.astype(jnp.bfloat16), 'head', scatter_dime...]
    all_gather x4 -> x0, blocking collectives: 51.5 us -> none  [the longest x1 14.6 us: body(): lax.all_gather(audio_mixed[:, 2 * cross_width:], 'ctx', axis=0, tiled=True)]
    ppermute x0 -> x15, starting transfers between devices: none -> 35 us  [shift(): return lax.ppermute(value, 'ctx', ring)]
    unnamed x22 -> x25, local copies, waits for them, and re-layouts: 33.9 us -> 4.29 us
    reduce_sum x5, other arithmetic: 21.1 us -> 3 us  [the longest x1 1.43 us: fast_body(): jnp.sum(video_wide * video_wide, axis=1)]
  transfers between devices with their start and end apart: 7 -> 15, of which waited for: 4 -> 4; matrix products, arithmetic and copies ran while one was open for 33% -> 4% of each run, Pallas kernels for 0% -> 29%
where the time goes in v1:
time: 228 us; the launch traced here: 227 us
  Pallas kernels  156 us (68%)
  starting transfers between devices  35 us (15%)
  local copies, waits for them, and re-layouts  14.7 us (6%)
  waiting for transfers between devices  9.59 us (4%)
  other arithmetic  6.31 us (3%)
  matrix products  4.6 us (2%)
    pallas_call x2, Pallas kernels, project(): pl.pallas_call(functools.partial(project_kernel, heads), grid=(blocks.sha...  38.5 us
    pallas_call x1, Pallas kernels, gather_blocks(): pl.pallas_call(gather_kernel, out_shape=(jax.ShapeDtypeStruct((8,) + bloc...  36.8 us
    pallas_call x1, Pallas kernels, scatter_blocks(): pl.pallas_call(scatter_kernel, out_shape=jax.ShapeDtypeStruct(base.shape,...  36.4 us
    ppermute x15, starting transfers between devices, shift(): return lax.ppermute(value, 'ctx', ring)  35 us
    pallas_call x4, Pallas kernels, self_attention(): pl.pallas_call(functools.partial(attention_kernel, count), grid=(heads, r...  27.2 us
    pallas_call x1, Pallas kernels, output_parts(): pl.pallas_call(output_kernel, grid=(8,), out_shape=jax.ShapeDtypeStruct((...  11.1 us
    ppermute x15, waiting for transfers between devices, shift(): return lax.ppermute(value, 'ctx', ring)  9.59 us
    pallas_call x1, Pallas kernels, cross_attention(): pl.pallas_call(functools.partial(cross_kernel, count), out_shape=(jax.Sha...  5.88 us
  transfers between devices with their start and end apart: 15, of which 4 were waited for; matrix products, arithmetic and copies ran while one was open for 4% of the time, Pallas kernels for 29%

profile of v1, /device:TPU:0, one launch (start us, length us, event | category | flops | bytes accessed | tf_op | source)
XLA Modules:
  0.0 227.0 jit_solution(17245192593431029136)
XLA Ops:
  0.6 0.9 fusion.12
  1.6 1.4 fusion.1
  3.0 0.6 fusion.14.sq_ref
  3.6 1.0 maximum_maximum_fusion.x_ref
  4.6 36.8 %gather_blocks.1 = (bf16[8,816,512]{2,1,0:T(8,128)(2,1)}, f32[8,8,128]{2,1,0:T(8,128)}) custom-call(bf16[816,512]{1,0:T(8,128)(2,1)} %maximum_maximum_fusion.x_ref, f32[8,128]{1,0:T(8,128)} %fusion.14.sq_ref), custom_call_target="tpu_custom_call" | custom-call | tf_op jit(solution)/shard_map/gather_blocks/pallas_call | solution.py:260
  41.3 1.0 slice.82
  42.8 1.5 fusion.2
  44.4 1.5 fusion.3
  45.9 1.5 fusion.4
  47.5 1.6 collective-permute-start.6
  49.1 2.6 %collective-permute-start.7 = (bf16[96,768]{1,0:T(8,128)(2,1)S(1)}, bf16[96,768]{1,0:T(8,128)(2,1)}, u32[]{:S(2)}, u32[]{:S(2)}) collective-permute-start(bf16[96,768]{1,0:T(8,128)(2,1)S(1)} %pad_maximum_fusion.refs_0_), channel_id=1, source_target_pairs={{0,16},{8,24},{16,0},{24,8},{1,17},{9,25},{17,1},{25,9},{2,18},{10... | collective-permute-start | bytes 442376 | tf_op jit(solution)/shard_map/ppermute | solution.py:579
  51.7 1.3 collective-permute-start.8
  53.0 0.9 copy.43
  54.0 21.6 %project.2 = bf16[4,3,768,128]{3,2,1,0:T(8,128)(2,1)} custom-call(bf16[8,816,512]{2,1,0:T(8,128)(2,1)} %get-tuple-element.7.x_ref, bf16[3,4096,512]{2,1,0:T(8,128)(2,1)} %bitcast.92, f32[768,1]{1,0:T(8,128)} %bitcast.78), custom_call_target="tpu_custom_call" | custom-call | flops 9663676416 | bytes 12582912 | tf_op jit(solution)/shard_map/project/pallas_call | solution.py:391
  75.6 2.6 %constant_dynamic-slice_fusion = (bf16[1,3,768,128]{3,2,1,0:T(8,128)(2,1)S(1)}, bf16[1,3,768,128]{3,2,1,0:T(8,128)(2,1)S(1)}, bf16[1,3,768,128]{3,2,1,0:T(8,128)(2,1)S(1)}, bf16[1,3,768,128]{3,2,1,0:T(8,128)(2,1)}) fusion(bf16[4,3,768,128]{3,2,1,0:T(8,128)(2,1)} %project.2, s32[]{:T(128)S(6)} %select_n.46, s32[]{:T(128)S(6)} %select_n.44, s32[]{:T(128)S(6)} %select_n.42, ...), kind=kLoop, calls=%fused_computation.67 | loop fusion | bytes 4718608 | tf_op jit(solution)/shard_map/jit(dynamic_index_in_dim)/squeeze | solution.py:597
  78.2 0.7 collective-permute-start
  79.2 16.9 %project.3.video_ref = bf16[2,3,768,128]{3,2,1,0:T(8,128)(2,1)} custom-call(bf16[8,816,512]{2,1,0:T(8,128)(2,1)} %get-tuple-element.7.x_ref, bf16[3,4096,256]{2,1,0:T(8,128)(2,1)} %bitcast.93, f32[768,1]{1,0:T(8,128)} %bitcast.79), custom_call_target="tpu_custom_call" | custom-call | flops 4831838208 | bytes 6291456 | tf_op jit(solution)/shard_map/project/pallas_call | solution.py:391
  96.1 1.1 maximum_maximum_fusion.1.base_ref
  97.2 0.6 copy-done.6
  97.8 5.9 %cross_attention.1 = (bf16[768,256]{1,0:T(8,128)(2,1)}, bf16[4,96,256]{2,1,0:T(8,128)(2,1)}, f32[4,2,96,128]{3,2,1,0:T(8,128)}) custom-call(bf16[2,3,768,128]{3,2,1,0:T(8,128)(2,1)} %project.3.video_ref, bf16[96,768]{1,0:T(8,128)(2,1)} %copy-done.3, bf16[96,768]{1,0:T(8,128)(2,1)} %copy-done.6, bf16[96,768]{1,0:T(8,128)(2,1)} %collective-permute-done.7.refs_2_, ...), custom_call_target="tpu_custom_call" | custom-call | flops 1207959552 | bytes 1572864 | tf_op jit(solution)/shard_map/cross_attention/pallas_call | solution.py:490
  103.7 1.6 slice_reduce_fusion.1
  105.3 2.9 %collective-permute-start.12 = (f32[2,2,96]{2,1,0:T(2,128)S(1)}, f32[2,2,96]{2,1,0:T(2,128)S(1)}, u32[]{:S(2)}, u32[]{:S(2)}) collective-permute-start(f32[2,2,96]{2,1,0:T(2,128)S(1)} %get-tuple-element.35), channel_id=1, source_target_pairs={{0,24},{8,0},{16,8},{24,16},{1,25},{9,1},{17,9},{25,17},{2,26},{10... | collective-permute-start | bytes 4616 | tf_op jit(solution)/shard_map/ppermute | solution.py:579
  108.2 2.0 collective-permute-start.13
  110.2 0.9 fusion.26
  111.1 3.9 %collective-permute-start.2 = (bf16[1,3,768,128]{3,2,1,0:T(8,128)(2,1)S(1)}, bf16[1,3,768,128]{3,2,1,0:T(8,128)(2,1)}, u32[]{:S(2)}, u32[]{:S(2)}) collective-permute-start(bf16[1,3,768,128]{3,2,1,0:T(8,128)(2,1)S(1)} %get-tuple-element.16), channel_id=1, source_target_pairs={{0,24},{8,0},{16,8},{24,16},{1,25},{9,1},{17,9},{25,17},{2,26},{10... | collective-permute-start | bytes 1769480 | tf_op jit(solution)/shard_map/ppermute | solution.py:579
  115.0 4.8 %collective-permute-done.13 = f32[2,2,96]{2,1,0:T(2,128)S(1)} collective-permute-done((f32[2,2,96]{2,1,0:T(2,128)S(1)}, f32[2,2,96]{2,1,0:T(2,128)S(1)}, u32[]{:S(2)}, u32[]{:S(2)}) %collective-permute-start.13) | collective-permute-done | bytes 1568 | tf_op jit(solution)/shard_map/ppermute | solution.py:579
  119.8 12.7 %collective-permute-start.9 = (bf16[96,256]{1,0:T(8,128)(2,1)S(1)}, bf16[96,256]{1,0:T(8,128)(2,1)S(1)}, u32[]{:S(2)}, u32[]{:S(2)}) collective-permute-start(bf16[96,256]{1,0:T(8,128)(2,1)S(1)} %get-tuple-element.27), channel_id=1, source_target_pairs={{0,24},{8,0},{16,8},{24,16},{1,25},{9,1},{17,9},{25,17},{2,26},{10... | collective-permute-start | bytes 147464 | tf_op jit(solution)/shard_map/ppermute | solution.py:579
  132.6 1.7 collective-permute-done.9
  134.3 3.1 %collective-permute-start.11 = (bf16[96,256]{1,0:T(8,128)(2,1)S(1)}, bf16[96,256]{1,0:T(8,128)(2,1)S(1)}, u32[]{:S(2)}, u32[]{:S(2)}) collective-permute-start(bf16[96,256]{1,0:T(8,128)(2,1)S(1)} %get-tuple-element.25), channel_id=1, source_target_pairs={{0,8},{8,16},{16,24},{24,0},{1,9},{9,17},{17,25},{25,1},{2,10},{10... | collective-permute-start | bytes 147464 | tf_op jit(solution)/shard_map/ppermute | solution.py:579
  137.5 0.5 collective-permute-done.10
  138.1 2.5 %collective-permute-done.11 = bf16[96,256]{1,0:T(8,128)(2,1)S(1)} collective-permute-done((bf16[96,256]{1,0:T(8,128)(2,1)S(1)}, bf16[96,256]{1,0:T(8,128)(2,1)S(1)}, u32[]{:S(2)}, u32[]{:S(2)}) %collective-permute-start.11) | collective-permute-done | bytes 49184 | tf_op jit(solution)/shard_map/ppermute | solution.py:579
  140.6 0.6 multiply_reduce_fusion
  141.2 0.6 copy.49
  141.9 0.8 copy-done.5
  142.7 6.8 %self_attention.7 = bf16[1,768,128]{2,1,0:T(8,128)(2,1)} custom-call(bf16[1,3,768,128]{3,2,1,0:T(8,128)(2,1)} %collective-permute-done.2.refs_3_.refs_7_.q_ref, bf16[1,3,768,128]{3,2,1,0:T(8,128)(2,1)} %get-tuple-element.19.q_ref.refs_0_.refs_4_, bf16[1,3,768,128]{3,2,1,0:T(8,128)(2,1)} %copy-done.5, ...), custom_call_target="tpu_custom_call" | custom-call | flops 2415919104 | bytes 1572864 | tf_op jit(solution)/shard_map/self_attention/pallas_call | solution.py:446
  149.5 0.9 collective-permute-start.5
  150.3 6.8 %self_attention.6 = bf16[1,768,128]{2,1,0:T(8,128)(2,1)} custom-call(bf16[1,3,768,128]{3,2,1,0:T(8,128)(2,1)} %collective-permute-done.1.refs_2_.refs_6_.q_ref, bf16[1,3,768,128]{3,2,1,0:T(8,128)(2,1)} %get-tuple-element.19.q_ref.refs_0_.refs_4_, bf16[1,3,768,128]{3,2,1,0:T(8,128)(2,1)} %copy-done.5, ...), custom_call_target="tpu_custom_call" | custom-call | flops 2415919104 | bytes 1572864 | tf_op jit(solution)/shard_map/self_attention/pallas_call | solution.py:446
  157.1 1.7 collective-permute-start.4
  158.9 6.8 %self_attention.5 = bf16[1,768,128]{2,1,0:T(8,128)(2,1)} custom-call(bf16[1,3,768,128]{3,2,1,0:T(8,128)(2,1)} %copy-done.5, bf16[1,3,768,128]{3,2,1,0:T(8,128)(2,1)} %get-tuple-element.19.q_ref.refs_0_.refs_4_, bf16[1,3,768,128]{3,2,1,0:T(8,128)(2,1)} %copy-done.5, bf16[1,3,768,128]{3,2,1,0:T(8,128)(2,1)} %collective-permute-done.1.refs_2_.refs_6_.q_ref, ...), custom_call_target="tpu_custom_call" | custom-call | flops 2415919104 | bytes 1572864 | tf_op jit(solution)/shard_map/self_attention/pallas_call | solution.py:446
  165.7 1.3 collective-permute-start.3
  166.9 6.8 %self_attention.4 = bf16[1,768,128]{2,1,0:T(8,128)(2,1)} custom-call(bf16[1,3,768,128]{3,2,1,0:T(8,128)(2,1)} %get-tuple-element.19.q_ref.refs_0_.refs_4_, bf16[1,3,768,128]{3,2,1,0:T(8,128)(2,1)} %get-tuple-element.19.q_ref.refs_0_.refs_4_, bf16[1,3,768,128]{3,2,1,0:T(8,128)(2,1)} %copy-done.5, ...), custom_call_target="tpu_custom_call" | custom-call | flops 2415919104 | bytes 1572864 | tf_op jit(solution)/shard_map/self_attention/pallas_call | solution.py:446
  173.7 1.0 constant_dynamic-update-slice_fusion.7
  175.0 1.0 copy_bitcast_fusion.self_ref
  176.0 11.1 %output_parts.1.part_ref = bf16[8,816,512]{2,1,0:T(8,128)(2,1)} custom-call(bf16[768,512]{1,0:T(8,128)(2,1)} %copy_bitcast_fusion.self_ref, bf16[768,256]{1,0:T(8,128)(2,1)} %get-tuple-element.9.cross_ref, bf16[96,256]{1,0:T(8,128)(2,1)} %bitcast.83, bf16[512,4096]{1,0:T(8,128)(2,1)} %w_self.1, bf16[256,4096]{1,0:T(8,128)(2,1)} %w_cross.1, ...), custom_call_target="tpu_custom_call" | custom-call | tf_op jit(solution)/shard_map/output_parts/pallas_call | solution.py:527
  187.1 36.4 %scatter_blocks.1 = bf16[816,512]{1,0:T(8,128)(2,1)} custom-call(bf16[8,816,512]{2,1,0:T(8,128)(2,1)} %output_parts.1.part_ref, bf16[816,512]{1,0:T(8,128)(2,1)} %maximum_maximum_fusion.1.base_ref), custom_call_target="tpu_custom_call" | custom-call | tf_op jit(solution)/shard_map/scatter_blocks/pallas_call | solution.py:344
  223.5 0.8 fusion.25
  224.3 2.1 slice.101
  226.4 0.6 pad_maximum_fusion.1
  (53 shorter events, 1.3 us)
Async XLA Ops:
  41.3 1.5 copy-start.4
  47.5 28.2 %copy-start.3 = (bf16[96,768]{1,0:T(8,128)(2,1)}, bf16[96,768]{1,0:T(8,128)(2,1)S(1)}, u32[]{:S(2)}) copy-start(bf16[96,768]{1,0:T(8,128)(2,1)S(1)} %pad_maximum_fusion.refs_0_) | copy-start | bytes 442372
  47.5 49.7 %collective-permute-start.6 = (bf16[96,768]{1,0:T(8,128)(2,1)S(1)}, bf16[96,768]{1,0:T(8,128)(2,1)S(1)}, u32[]{:S(2)}, u32[]{:S(2)}) collective-permute-start(bf16[96,768]{1,0:T(8,128)(2,1)S(1)} %pad_maximum_fusion.refs_0_), channel_id=1, source_target_pairs={{0,8},{8,16},{16,24},{24,0},{1,9},{9,17},{17,25},{25,1},{2,10},{10... | collective-permute-start | bytes 442376 | tf_op jit(solution)/shard_map/ppermute | solution.py:579
  49.1 48.1 %collective-permute-start.7 = (bf16[96,768]{1,0:T(8,128)(2,1)S(1)}, bf16[96,768]{1,0:T(8,128)(2,1)}, u32[]{:S(2)}, u32[]{:S(2)}) collective-permute-start(bf16[96,768]{1,0:T(8,128)(2,1)S(1)} %pad_maximum_fusion.refs_0_), channel_id=1, source_target_pairs={{0,16},{8,24},{16,0},{24,8},{1,17},{9,25},{17,1},{25,9},{2,18},{10... | collective-permute-start | bytes 442376 | tf_op jit(solution)/shard_map/ppermute | solution.py:579
  51.7 45.5 %collective-permute-start.8 = (bf16[96,768]{1,0:T(8,128)(2,1)S(1)}, bf16[96,768]{1,0:T(8,128)(2,1)}, u32[]{:S(2)}, u32[]{:S(2)}) collective-permute-start(bf16[96,768]{1,0:T(8,128)(2,1)S(1)} %pad_maximum_fusion.refs_0_), channel_id=1, source_target_pairs={{0,24},{8,0},{16,8},{24,16},{1,25},{9,1},{17,9},{25,17},{2,26},{10... | collective-permute-start | bytes 442376 | tf_op jit(solution)/shard_map/ppermute | solution.py:579
  78.2 63.7 %collective-permute-start = (bf16[1,3,768,128]{3,2,1,0:T(8,128)(2,1)S(1)}, bf16[1,3,768,128]{3,2,1,0:T(8,128)(2,1)S(1)}, u32[]{:S(2)}, u32[]{:S(2)}) collective-permute-start(bf16[1,3,768,128]{3,2,1,0:T(8,128)(2,1)S(1)} %get-tuple-element.18), channel_id=1, source_target_pairs={{0,8},{8,16},{16,24},{24,0},{1,9},{9,17},{17,25},{25,1},{2,10},{10... | collective-permute-start | bytes 1769480 | tf_op jit(solution)/shard_map/ppermute | solution.py:579
  78.8 63.0 %collective-permute-start.1 = (bf16[1,3,768,128]{3,2,1,0:T(8,128)(2,1)S(1)}, bf16[1,3,768,128]{3,2,1,0:T(8,128)(2,1)}, u32[]{:S(2)}, u32[]{:S(2)}) collective-permute-start(bf16[1,3,768,128]{3,2,1,0:T(8,128)(2,1)S(1)} %get-tuple-element.17), channel_id=1, source_target_pairs={{0,16},{8,24},{16,0},{24,8},{1,17},{9,25},{17,1},{25,9},{2,18},{10... | collective-permute-start | bytes 1769480 | tf_op jit(solution)/shard_map/ppermute | solution.py:579
  79.2 16.9 %copy-start.2 = (bf16[96,256]{1,0:T(8,128)(2,1)S(1)}, bf16[96,256]{1,0:T(8,128)(2,1)}, u32[]{:S(2)}) copy-start(bf16[96,256]{1,0:T(8,128)(2,1)} %param.11) | copy-start | bytes 147460
  79.2 16.9 %copy-start = (bf16[768,512]{1,0:T(8,128)(2,1)S(1)}, bf16[768,512]{1,0:T(8,128)(2,1)}, u32[]{:S(2)}) copy-start(bf16[768,512]{1,0:T(8,128)(2,1)} %param.10) | copy-start | bytes 2359300
  97.2 0.7 copy-start.6
  105.3 5.8 %collective-permute-start.12 = (f32[2,2,96]{2,1,0:T(2,128)S(1)}, f32[2,2,96]{2,1,0:T(2,128)S(1)}, u32[]{:S(2)}, u32[]{:S(2)}) collective-permute-start(f32[2,2,96]{2,1,0:T(2,128)S(1)} %get-tuple-element.35), channel_id=1, source_target_pairs={{0,24},{8,0},{16,8},{24,16},{1,25},{9,1},{17,9},{25,17},{2,26},{10... | collective-permute-start | bytes 4616 | tf_op jit(solution)/shard_map/ppermute | solution.py:579
  108.2 11.6 %collective-permute-start.13 = (f32[2,2,96]{2,1,0:T(2,128)S(1)}, f32[2,2,96]{2,1,0:T(2,128)S(1)}, u32[]{:S(2)}, u32[]{:S(2)}) collective-permute-start(f32[2,2,96]{2,1,0:T(2,128)S(1)} %get-tuple-element.37), channel_id=1, source_target_pairs={{0,16},{8,24},{16,0},{24,8},{1,17},{9,25},{17,1},{25,9},{2,18},{10... | collective-permute-start | bytes 4616 | tf_op jit(solution)/shard_map/ppermute | solution.py:579
  110.2 22.3 %collective-permute-start.14 = (f32[2,2,96]{2,1,0:T(2,128)S(1)}, f32[2,2,96]{2,1,0:T(2,128)S(1)}, u32[]{:S(2)}, u32[]{:S(2)}) collective-permute-start(f32[2,2,96]{2,1,0:T(2,128)S(1)} %get-tuple-element.36), channel_id=1, source_target_pairs={{0,8},{8,16},{16,24},{24,0},{1,9},{9,17},{17,25},{25,1},{2,10},{10... | collective-permute-start | bytes 4616 | tf_op jit(solution)/shard_map/ppermute | solution.py:579
  111.1 30.8 %collective-permute-start.2 = (bf16[1,3,768,128]{3,2,1,0:T(8,128)(2,1)S(1)}, bf16[1,3,768,128]{3,2,1,0:T(8,128)(2,1)}, u32[]{:S(2)}, u32[]{:S(2)}) collective-permute-start(bf16[1,3,768,128]{3,2,1,0:T(8,128)(2,1)S(1)} %get-tuple-element.16), channel_id=1, source_target_pairs={{0,24},{8,0},{16,8},{24,16},{1,25},{9,1},{17,9},{25,17},{2,26},{10... | collective-permute-start | bytes 1769480 | tf_op jit(solution)/shard_map/ppermute | solution.py:579
  119.8 14.5 %collective-permute-start.9 = (bf16[96,256]{1,0:T(8,128)(2,1)S(1)}, bf16[96,256]{1,0:T(8,128)(2,1)S(1)}, u32[]{:S(2)}, u32[]{:S(2)}) collective-permute-start(bf16[96,256]{1,0:T(8,128)(2,1)S(1)} %get-tuple-element.27), channel_id=1, source_target_pairs={{0,24},{8,0},{16,8},{24,16},{1,25},{9,1},{17,9},{25,17},{2,26},{10... | collective-permute-start | bytes 147464 | tf_op jit(solution)/shard_map/ppermute | solution.py:579
  132.5 5.5 %collective-permute-start.10 = (bf16[96,256]{1,0:T(8,128)(2,1)S(1)}, bf16[96,256]{1,0:T(8,128)(2,1)S(1)}, u32[]{:S(2)}, u32[]{:S(2)}) collective-permute-start(bf16[96,256]{1,0:T(8,128)(2,1)S(1)} %get-tuple-element.26), channel_id=1, source_target_pairs={{0,16},{8,24},{16,0},{24,8},{1,17},{9,25},{17,1},{25,9},{2,18},{10... | collective-permute-start | bytes 147464 | tf_op jit(solution)/shard_map/ppermute | solution.py:579
  134.3 6.3 %collective-permute-start.11 = (bf16[96,256]{1,0:T(8,128)(2,1)S(1)}, bf16[96,256]{1,0:T(8,128)(2,1)S(1)}, u32[]{:S(2)}, u32[]{:S(2)}) collective-permute-start(bf16[96,256]{1,0:T(8,128)(2,1)S(1)} %get-tuple-element.25), channel_id=1, source_target_pairs={{0,8},{8,16},{16,24},{24,0},{1,9},{9,17},{17,25},{25,1},{2,10},{10... | collective-permute-start | bytes 147464 | tf_op jit(solution)/shard_map/ppermute | solution.py:579
  141.8 0.8 copy-start.5
  149.5 25.4 %collective-permute-start.5 = (bf16[1,768,128]{2,1,0:T(8,128)(2,1)}, bf16[1,768,128]{2,1,0:T(8,128)(2,1)S(1)}, u32[]{:S(2)}, u32[]{:S(2)}) collective-permute-start(bf16[1,768,128]{2,1,0:T(8,128)(2,1)} %self_attention.7), channel_id=1, source_target_pairs={{0,8},{8,16},{16,24},{24,0},{1,9},{9,17},{17,25},{25,1},{2,10},{10... | collective-permute-start | bytes 589832 | tf_op jit(solution)/shard_map/ppermute | solution.py:579
  157.1 17.7 %collective-permute-start.4 = (bf16[1,768,128]{2,1,0:T(8,128)(2,1)}, bf16[1,768,128]{2,1,0:T(8,128)(2,1)S(1)}, u32[]{:S(2)}, u32[]{:S(2)}) collective-permute-start(bf16[1,768,128]{2,1,0:T(8,128)(2,1)} %self_attention.6), channel_id=1, source_target_pairs={{0,16},{8,24},{16,0},{24,8},{1,17},{9,25},{17,1},{25,9},{2,18},{10... | collective-permute-start | bytes 589832 | tf_op jit(solution)/shard_map/ppermute | solution.py:579
  165.7 9.1 %collective-permute-start.3 = (bf16[1,768,128]{2,1,0:T(8,128)(2,1)}, bf16[1,768,128]{2,1,0:T(8,128)(2,1)S(1)}, u32[]{:S(2)}, u32[]{:S(2)}) collective-permute-start(bf16[1,768,128]{2,1,0:T(8,128)(2,1)} %self_attention.5), channel_id=1, source_target_pairs={{0,24},{8,0},{16,8},{24,16},{1,25},{9,1},{17,9},{25,17},{2,26},{10... | collective-permute-start | bytes 589832 | tf_op jit(solution)/shard_map/ppermute | solution.py:579
  173.7 1.2 copy-start.1
